TPU v7x, 32 devices: a whole 2x2x4 slice. The times are simulated.
32 devices in a mesh: dp: 8 (over z, y), tensor: 4 (over x, core).
Axes of the slice: x: 2, y: 2, z: 4, core: 2. Of those that a mesh axis runs over, the one named last changes fastest.
Arguments:
- acts: bfloat16 [8192, 5120], P('dp', 'tensor'), may hold values from -6 to 6
- out_grad: bfloat16 [8192, 2048], P(('dp', 'tensor')), may hold values from -0.1875 to 0.1875
- momentum: float32 [40960, 2048], P(('dp', 'tensor')), may hold values from -100 to 100
- q_basis: float32 [2048, 256], P('tensor'), may hold values from -0.125 to 0.125
Outputs:
- new_momentum: float32 [40960, 2048], P(('dp', 'tensor'))
- ortho: float32 [5120, 256], P('tensor')
- new_q: float32 [2048, 256], P('tensor')
All inputs are finite; a program needn't handle non-finite values.
Results may differ from a plain program's by a relative error of at most 0.0003.
Values may be sent and summed in bfloat16 or wider, within the bound.
No kernel may reach another device: no remote copies, remote signals or barrier semaphores. Data moves between devices by JAX's collectives and lax.ppermute only.
A program may use at most 64 MiB of HBM per device.

v0:
```python
import jax
import jax.numpy as jnp
from jax import lax
from jax.sharding import PartitionSpec as P

HIGH = lax.Precision.HIGHEST


def contract_rows(first, second):
    return lax.dot_general(
        first, second, (((0,), (0,)), ((), ())), precision=HIGH, preferred_element_type=jnp.float32
    )


def orthonormal(left, gram):
    chol = jnp.linalg.cholesky(gram)
    return lax.linalg.triangular_solve(chol, left, left_side=False, lower=True, transpose_a=True)


def body(acts, out_grad, momentum, q_basis):
    replicas = lax.axis_size("dp")
    grad = lax.dot_general(
        acts,
        lax.all_gather(out_grad, "tensor", axis=0, tiled=True),
        (((0,), (0,)), ((), ())),
        preferred_element_type=jnp.float32,
    )
    buffer = 0.95 * momentum + grad
    columns = buffer
    left_local = jnp.dot(
        columns,
        lax.all_gather(q_basis, "tensor", axis=0, tiled=True),
        precision=HIGH,
        preferred_element_type=jnp.float32,
    )
    left = lax.psum(left_local, "dp") / replicas
    gram = lax.psum(contract_rows(left, left), "tensor")
    ortho = orthonormal(left, gram)
    columns = buffer
    right_share = lax.psum_scatter(
        contract_rows(columns, ortho), "tensor", scatter_dimension=0, tiled=True
    )
    right_share = lax.psum(right_share, "dp") / replicas
    col_squares = lax.psum(jnp.sum(right_share * right_share, axis=0, keepdims=True), "tensor")
    new_q = right_share * lax.rsqrt(col_squares + 1e-06)
    columns = buffer
    update = lax.dot_general(
        ortho,
        lax.all_gather(right_share.astype(jnp.bfloat16), "tensor", axis=0, tiled=True).astype(
            jnp.float32
        ),
        (((1,), (1,)), ((), ())),
        precision=HIGH,
        preferred_element_type=jnp.float32,
    )
    new_momentum = columns - 0.05 * update
    return (new_momentum, ortho, new_q)


def solution(mesh):
    in_specs = (
        P("dp", "tensor"),
        P(("dp", "tensor"), None),
        P(("dp", "tensor"), None),
        P("tensor", None),
    )
    out_specs = (P(("dp", "tensor"), None), P("tensor", None), P("tensor", None))
    return jax.shard_map(body, mesh=mesh, in_specs=in_specs, out_specs=out_specs, check_vma=False)
```

profile of v0, /device:TPU:0, one launch (start us, length us, event | category | flops | bytes accessed | tf_op | source)
XLA Modules:
  0.0 450.5 jit_solution(18422451597590470659)
XLA Ops:
  7.2 0.0 all-gather.4.cloned.1.call-start
  7.2 0.7 all-gather.4.cloned.1.call-update
  7.9 0.0 all-gather.6.cloned.1.call-start
  8.0 0.7 all-gather.6.cloned.1.call-update
  8.7 0.0 all-reduce.5.cloned.1.call-start
  8.7 38.0 %all-gather.4.cloned.1.call-done = bf16[1024,2048]{1,0:T(8,128)(2,1)} async-done(((bf16[256,2048]{1,0:T(8,128)(2,1)}), bf16[1024,2048]{1,0:T(8,128)(2,1)}) %all-gather.4.cloned.1.call-update) | async-done | bytes 4194320 | tf_op jit(solution)/shard_map/all_gather | solution.py:24
  46.8 12.1 %multiply_add_fusion = f32[1280,2048]{1,0:T(8,128)} fusion(f32[1280,2048]{1,0:T(8,128)} %param.6, bf16[1024,1280]{1,0:T(8,128)(2,1)S(1)} %copy-done, bf16[1024,2048]{1,0:T(8,128)(2,1)} %all-gather.4.cloned.1.call-done), kind=kOutput, calls=%fused_computation.3 | convolution fusion | flops 5373952000 | bytes 27787264 | tf_op jit(solution)/shard_map/dot_general | solution.py:22
  58.9 12.0 %all-gather.6.cloned.1.call-done = f32[2048,256]{1,0:T(8,128)} async-done(((f32[512,256]{1,0:T(8,128)}), f32[2048,256]{1,0:T(8,128)}) %all-gather.6.cloned.1.call-update) | async-done | bytes 2097168 | tf_op jit(solution)/shard_map/all_gather | solution.py:32
  70.9 12.5 %fusion.11 = f32[1280,256]{1,0:T(8,128)} fusion(f32[1280,2048]{1,0:T(8,128)} %multiply_add_fusion, f32[2048,256]{1,0:T(8,128)} %all-gather.6.cloned.1.call-done), kind=kOutput, calls=%fused_computation.38 | convolution fusion | flops 8053063680 | bytes 13893632 | tf_op jit(solution)/shard_map/dot_general | solution.py:30
  83.4 0.0 all-reduce.5.cloned.1.call-update
  83.4 0.0 all-reduce.7.cloned.1.call-start
  83.5 83.7 %all-reduce.5.cloned.1.call-done = f32[1280,256]{1,0:T(8,128)} async-done(((f32[1280,256]{1,0:T(8,128)}), f32[1280,256]{1,0:T(8,128)}) %all-reduce.5.cloned.1.call-update) | async-done | bytes 1310736 | tf_op jit(solution)/shard_map/psum | solution.py:36
  167.2 4.8 %fusion.8 = f32[256,256]{0,1:T(8,128)} fusion(f32[1280,256]{1,0:T(8,128)} %all-reduce.5.cloned.1.call-done), kind=kOutput, calls=%fused_computation.35 | convolution fusion | flops 1006960640 | bytes 1572864 | tf_op jit(solution)/shard_map/dot_general | solution.py:10
  172.0 0.5 reduce-scatter.2.cloned.1.call-start
  172.5 2.5 broadcast_multiply_fusion
  175.0 28.5 %all-reduce.7.cloned.1.call-done = f32[256,256]{0,1:T(8,128)} async-done(((f32[256,256]{0,1:T(8,128)}), f32[256,256]{0,1:T(8,128)}) %all-reduce.7.cloned.1.call-update) | async-done | bytes 262160 | tf_op jit(solution)/shard_map/psum | solution.py:37
  203.5 1.1 copy.8
  204.6 1.0 fusion.2
  205.6 11.7 %cholesky.50 = f32[128,128]{1,0:T(8,128)S(1)} custom-call(f32[128,128]{1,0:T(8,128)S(1)} %cholesky.118), custom_call_target="Cholesky" | custom-call | tf_op jit(solution)/shard_map/jit(cholesky)/cholesky | solution.py:16
  217.4 9.8 %custom-call.14 = f32[1,128,128]{1,2,0:T(8,128)S(1)} custom-call(f32[1,128,128]{2,1,0:T(8,128)S(1)} %get-tuple-element.29), custom_call_target="InvertDiagBlocksLowerTriangular" | custom-call | tf_op jit(solution)/shard_map/jit(cholesky)/cholesky | solution.py:16
  227.2 0.2 constant_dynamic-update-slice_fusion.1
  227.4 0.3 convolution_subtract_fusion.1
  227.7 11.7 %cholesky.105 = f32[128,128]{1,0:T(8,128)S(1)} custom-call(f32[128,128]{1,0:T(8,128)S(1)} %convolution_subtract_fusion.1), custom_call_target="Cholesky" | custom-call | tf_op jit(solution)/shard_map/jit(cholesky)/cholesky | solution.py:16
  239.4 0.7 compare_reduce_fusion
  241.4 0.1 triangular_solve.58
  241.5 5.3 %while.1 = (s32[]{:T(128)}, f32[256,256]{1,0:T(8,128)S(1)}, s32[2,2]{1,0:T(2,128)S(1)}, f32[2,128,128]{2,1,0:T(8,128)}, s32[]{:T(128)}) while((s32[]{:T(128)}, f32[256,256]{1,0:T(8,128)S(1)}, s32[2,2]{1,0:T(2,128)S(1)}, f32[2,128,128]{2,1,0:T(8,128)}, s32[]{:T(128)}) %tuple.29), condition=%wide.while_cond, body=%wide.while_body.sunk | while | flops 2 | bytes 132205 | solution.py:17
  241.6 0.6 fusion.23
  242.2 2.0 bitcast_dynamic-update-slice_fusion.2
  244.2 0.6 fusion.23
  244.8 2.0 bitcast_dynamic-update-slice_fusion.2
  246.8 21.1 %custom-call.15 = f32[2,128,128]{1,2,0:T(8,128)} custom-call(f32[2,128,128]{2,1,0:T(8,128)} %get-tuple-element.10), custom_call_target="InvertDiagBlocksLowerTriangular" | custom-call | tf_op jit(solution)/shard_map/triangular_solve | solution.py:17
  267.9 1.8 fusion
  269.8 2.3 convolution_subtract_fusion
  272.1 0.7 fusion.3
  272.8 0.8 copy-done.1
  273.6 20.1 %fusion.9 = f32[2048,256]{1,0:T(8,128)} fusion(f32[1280,2048]{1,0:T(8,128)} %multiply_add_fusion, f32[1280,128]{0,1:T(8,128)S(1)} %fusion.3, f32[1280,128]{0,1:T(8,128)S(1)} %fusion), kind=kOutput, calls=%fused_computation.36 | convolution fusion | flops 8053391360 | bytes 13893632 | tf_op jit(solution)/shard_map/dot_general | solution.py:10
  293.8 0.0 all-reduce.9.cloned.1.call-start
  293.8 31.3 %reduce-scatter.2.cloned.1.call-done = f32[512,256]{1,0:T(8,128)} async-done(((f32[2048,256]{1,0:T(8,128)}), f32[512,256]{1,0:T(8,128)}) %reduce-scatter.2.cloned.1.call-update) | async-done | bytes 524304 | tf_op jit(solution)/shard_map/reduce_scatter | solution.py:40
  325.1 0.0 all-reduce.9.cloned.1.call-update
  325.1 0.0 all-gather.8.cloned.1.call-start
  325.2 76.0 %all-reduce.9.cloned.1.call-done = f32[512,256]{1,0:T(8,128)} async-done(((f32[512,256]{1,0:T(8,128)}), f32[512,256]{1,0:T(8,128)}) %all-reduce.9.cloned.1.call-update) | async-done | bytes 524304 | tf_op jit(solution)/shard_map/psum | solution.py:43
  401.2 1.1 multiply_reduce_fusion
  402.3 5.9 %psum.31 = f32[1,256]{1,0:T(1,128)S(1)} all-reduce(f32[1,256]{1,0:T(1,128)S(1)} %bitcast.39), channel_id=1, replica_groups=mesh['dp'=8,'tensor'=4] {'tensor'}, use_global_device_ids=true, to_apply=%region_9.10 | all-reduce | flops 256 | bytes 2048 | tf_op jit(solution)/shard_map/psum | solution.py:44
  408.2 2.0 broadcast_multiply_fusion.1
  410.2 2.2 pad_maximum_fusion
  412.5 2.8 copy.9
  415.2 11.3 %all-gather.8.cloned.1.call-done = bf16[2048,256]{1,0:T(8,128)(2,1)} async-done(((bf16[512,256]{1,0:T(8,128)(2,1)}), bf16[2048,256]{1,0:T(8,128)(2,1)}) %all-gather.8.cloned.1.call-update) | async-done | bytes 1048592 | tf_op jit(solution)/shard_map/all_gather | solution.py:49
  426.5 17.0 %multiply_subtract_fusion = f32[1280,2048]{1,0:T(8,128)} fusion(f32[1280,2048]{1,0:T(8,128)} %multiply_add_fusion, bf16[2048,256]{1,0:T(8,128)(2,1)} %all-gather.8.cloned.1.call-done, f32[1280,128]{0,1:T(8,128)} %copy-done.1, f32[1280,128]{0,1:T(8,128)S(1)} %fusion), kind=kOutput, calls=%fused_computation.2 | convolution fusion | flops 8058634240 | bytes 23330816 | tf_op jit(solution)/shard_map/dot_general | solution.py:47
  (18 shorter events, 0.2 us)
Async XLA Ops:
  7.2 39.6 %copy-start = (bf16[1024,1280]{1,0:T(8,128)(2,1)S(1)}, bf16[1024,1280]{1,0:T(8,128)(2,1)}, u32[]{:S(2)}) copy-start(bf16[1024,1280]{1,0:T(8,128)(2,1)} %param.4) | copy-start | bytes 7864324
  7.2 39.6 %all-gather.4.cloned.1.call-start = ((), (), s32[]{:S(2)}) async-start(), calls=%async_computation.1 | async-start | bytes 5242880 | tf_op jit(solution)/shard_map/all_gather | solution.py:24
  7.9 63.0 %all-gather.6.cloned.1.call-start = ((), (), s32[]{:S(2)}) async-start(), calls=%async_computation.2 | async-start | bytes 2621440 | tf_op jit(solution)/shard_map/all_gather | solution.py:32
  8.7 158.6 %all-reduce.5.cloned.1.call-start = ((), (), s32[]{:S(2)}) async-start(), calls=%async_computation.3 | async-start | bytes 2621440 | tf_op jit(solution)/shard_map/psum | solution.py:36
  83.4 120.1 %all-reduce.7.cloned.1.call-start = ((), (), s32[]{:S(2)}) async-start(), calls=%async_computation.4 | async-start | bytes 524288 | tf_op jit(solution)/shard_map/psum | solution.py:37
  172.0 153.1 %reduce-scatter.2.cloned.1.call-start = ((), (), s32[]{:S(2)}) async-start(), calls=%async_computation.5 | async-start | bytes 2621440 | tf_op jit(solution)/shard_map/reduce_scatter | solution.py:40
  267.9 4.2 copy-start.2
  272.8 0.8 copy-start.1
  293.8 107.4 %all-reduce.9.cloned.1.call-start = ((), (), s32[]{:S(2)}) async-start(), calls=%async_computation.6 | async-start | bytes 1048576 | tf_op jit(solution)/shard_map/psum | solution.py:43
  325.1 101.4 %all-gather.8.cloned.1.call-start = ((), (), s32[]{:S(2)}) async-start(), calls=%async_computation.7 | async-start | bytes 1310720 | tf_op jit(solution)/shard_map/all_gather | solution.py:49
Sparse Core Ops, SparseCore 0:
  9.5 37.1 all-gather.3
  48.3 22.5 all-gather.5
  83.5 83.6 all-reduce.4
  172.1 31.3 all-reduce.6
  293.9 31.1 reduce-scatter.1
  328.4 72.7 all-reduce.8
  410.3 16.1 all-gather.7
where the time goes:
time: 458 us; the launch traced here: 451 us
  waiting for transfers between devices  282 us (62%)
  matrix products  71.8 us (16%)
  other arithmetic  63.9 us (14%)
  between operations  15.8 us (3%)
  local copies, waits for them, and re-layouts  9.95 us (2%)
  blocking collectives  5.87 us (1%)
    psum x1, waiting for transfers between devices, body(): left = lax.psum(left_local, 'dp') / replicas  83.7 us
    psum x1, waiting for transfers between devices, body(): right_share = lax.psum(right_share, 'dp') / replicas  76 us
    all_gather x1, waiting for transfers between devices, body(): lax.all_gather(out_grad, 'tensor', axis=0, tiled=True)  38 us
    another operation x6, other arithmetic, orthonormal(): chol = jnp.linalg.cholesky(gram)  34 us
    reduce_scatter x1, waiting for transfers between devices, body(): lax.psum_scatter(contract_rows(columns, ortho), 'tensor', scatter_dimensi...  31.3 us
    psum x1, waiting for transfers between devices, body(): gram = lax.psum(contract_rows(left, left), 'tensor')  28.5 us
    dot_general x2, matrix products, contract_rows(): lax.dot_general(first, second, (((0,), (0,)), ((), ())), precision=HIGH,...  24.9 us
    another operation x4, other arithmetic, orthonormal(): lax.linalg.triangular_solve(chol, left, left_side=False, lower=True, tran...  23.4 us
  transfers between devices with their start and end apart: 7, of which 7 were waited for; matrix products, arithmetic and copies ran while one was open for 4% of the time, Pallas kernels for 0%

commit v1 on v0

--- a/solution.py
+++ b/solution.py
@@ -4,6 +4,11 @@
 from jax.sharding import PartitionSpec as P
 
 HIGH = lax.Precision.HIGHEST
+
+
+def pair_islands_on(xx, which_axis):
+    response = lax.all_gather(xx, which_axis)
+    return jnp.sum(response, 0)
 
 
 def contract_rows(first, second):
@@ -33,7 +38,7 @@
         precision=HIGH,
         preferred_element_type=jnp.float32,
     )
-    left = lax.psum(left_local, "dp") / replicas
+    left = pair_islands_on(left_local, "dp") / replicas
     gram = lax.psum(contract_rows(left, left), "tensor")
     ortho = orthonormal(left, gram)
     columns = buffer

time: 458 us -> 522 us (1.14)
  waiting for transfers between devices: 282 us -> 354 us
    all_gather x0 -> x1, waiting for transfers between devices: none -> 151 us  [pair_islands_on(): response = lax.all_gather(xx, which_axis)]
    psum x1 -> x0, waiting for transfers between devices: 83.7 us -> none  [body(): left = lax.psum(left_local, 'dp') / replicas]
  transfers between devices with their start and end apart: 7 -> 7, of which waited for: 7 -> 7; matrix products, arithmetic and copies ran while one was open for 4% -> 3% of each run, Pallas kernels for 0% -> 0%
where the time goes in v1:
time: 522 us; the launch traced here: 514 us
  waiting for transfers between devices  354 us (68%)
  matrix products  68.1 us (13%)
  other arithmetic  62.8 us (12%)
  between operations  15.8 us (3%)
  local copies, waits for them, and re-layouts  6.6 us (1%)
  blocking collectives  5.87 us (1%)
    all_gather x1, waiting for transfers between devices, pair_islands_on(): response = lax.all_gather(xx, which_axis)  151 us
    psum x1, waiting for transfers between devices, body(): right_share = lax.psum(right_share, 'dp') / replicas  75.9 us
    all_gather x1, waiting for transfers between devices, body(): lax.all_gather(out_grad, 'tensor', axis=0, tiled=True)  38 us
    another operation x6, other arithmetic, orthonormal(): chol = jnp.linalg.cholesky(gram)  33.9 us
    reduce_scatter x1, waiting for transfers between devices, body(): lax.psum_scatter(contract_rows(columns, ortho), 'tensor', scatter_dimensi...  31.3 us
    psum x1, waiting for transfers between devices, body(): gram = lax.psum(contract_rows(left, left), 'tensor')  30 us
    dot_general x2, matrix products, contract_rows(): lax.dot_general(first, second, (((0,), (0,)), ((), ())), precision=HIGH,...  23.3 us
    another operation x4, other arithmetic, orthonormal(): lax.linalg.triangular_solve(chol, left, left_side=False, lower=True, tran...  19.8 us
  transfers between devices with their start and end apart: 7, of which 7 were waited for; matrix products, arithmetic and copies ran while one was open for 3% of the time, Pallas kernels for 0%

profile of v1, /device:TPU:0, one launch (start us, length us, event | category | flops | bytes accessed | tf_op | source)
XLA Modules:
  0.0 514.1 jit_solution(8959229517802401319)
XLA Ops:
  7.2 0.0 all-gather.6.cloned.1.call-start
  7.2 0.7 all-gather.6.cloned.1.call-update
  7.9 0.0 all-gather.8.cloned.1.call-start
  8.0 0.7 all-gather.8.cloned.1.call-update
  8.7 0.0 all-gather.12.cloned.1.call-start
  8.7 38.0 %all-gather.6.cloned.1.call-done = bf16[1024,2048]{1,0:T(8,128)(2,1)} async-done(((bf16[256,2048]{1,0:T(8,128)(2,1)}), bf16[1024,2048]{1,0:T(8,128)(2,1)}) %all-gather.6.cloned.1.call-update) | async-done | bytes 4194320 | tf_op jit(solution)/shard_map/all_gather | solution.py:29
  46.8 12.2 %multiply_add_fusion = f32[1280,2048]{1,0:T(8,128)} fusion(f32[1280,2048]{1,0:T(8,128)} %param.6, bf16[1024,1280]{1,0:T(8,128)(2,1)S(1)} %copy-done, bf16[1024,2048]{1,0:T(8,128)(2,1)} %all-gather.6.cloned.1.call-done), kind=kOutput, calls=%fused_computation.3 | convolution fusion | flops 5373952000 | bytes 27787264 | tf_op jit(solution)/shard_map/dot_general | solution.py:27
  58.9 12.0 %all-gather.8.cloned.1.call-done = f32[2048,256]{1,0:T(8,128)} async-done(((f32[512,256]{1,0:T(8,128)}), f32[2048,256]{1,0:T(8,128)}) %all-gather.8.cloned.1.call-update) | async-done | bytes 2097168 | tf_op jit(solution)/shard_map/all_gather | solution.py:37
  70.9 12.5 %fusion.11 = f32[1280,256]{1,0:T(8,128)} fusion(f32[1280,2048]{1,0:T(8,128)} %multiply_add_fusion, f32[2048,256]{1,0:T(8,128)} %all-gather.8.cloned.1.call-done), kind=kOutput, calls=%fused_computation.38 | convolution fusion | flops 8053063680 | bytes 13893632 | tf_op jit(solution)/shard_map/dot_general | solution.py:35
  83.4 0.0 all-reduce.4.cloned.1.call-start
  83.5 150.6 %all-gather.12.cloned.1.call-done = f32[10240,256]{1,0:T(8,128)} async-done(((f32[1280,256]{1,0:T(8,128)}), f32[10240,256]{1,0:T(8,128)}) %all-gather.12.cloned.1.call-update) | async-done | bytes 10485776 | tf_op jit(solution)/shard_map/all_gather | solution.py:10
  234.1 4.8 reduce_sum.18
  238.9 3.0 fusion.8
  241.9 0.0 all-reduce.4.cloned.1.call-update
  241.9 0.5 reduce-scatter.2.cloned.1.call-start
  242.4 0.1 broadcast_multiply_fusion
  242.5 30.0 %all-reduce.4.cloned.1.call-done = f32[256,256]{0,1:T(8,128)} async-done(((f32[256,256]{0,1:T(8,128)}), f32[256,256]{0,1:T(8,128)}) %all-reduce.4.cloned.1.call-update) | async-done | bytes 262160 | tf_op jit(solution)/shard_map/psum | solution.py:42
  272.5 1.1 copy.8
  273.6 1.0 fusion.2
  274.6 11.7 %cholesky.50 = f32[128,128]{1,0:T(8,128)S(1)} custom-call(f32[128,128]{1,0:T(8,128)S(1)} %cholesky.118), custom_call_target="Cholesky" | custom-call | tf_op jit(solution)/shard_map/jit(cholesky)/cholesky | solution.py:21
  286.4 9.8 %custom-call.14 = f32[1,128,128]{1,2,0:T(8,128)S(1)} custom-call(f32[1,128,128]{2,1,0:T(8,128)S(1)} %get-tuple-element.29), custom_call_target="InvertDiagBlocksLowerTriangular" | custom-call | tf_op jit(solution)/shard_map/jit(cholesky)/cholesky | solution.py:21
  296.2 0.2 constant_dynamic-update-slice_fusion.1
  296.4 0.3 convolution_subtract_fusion.1
  296.7 11.7 %cholesky.105 = f32[128,128]{1,0:T(8,128)S(1)} custom-call(f32[128,128]{1,0:T(8,128)S(1)} %convolution_subtract_fusion.1), custom_call_target="Cholesky" | custom-call | tf_op jit(solution)/shard_map/jit(cholesky)/cholesky | solution.py:21
  308.4 0.6 compare_reduce_fusion
  310.4 0.1 triangular_solve.58
  310.5 4.2 while.1
  310.7 0.6 fusion.23
  311.3 1.4 bitcast_dynamic-update-slice_fusion.2
  312.7 0.6 fusion.23
  313.3 1.4 bitcast_dynamic-update-slice_fusion.2
  314.7 19.7 %custom-call.15 = f32[2,128,128]{1,2,0:T(8,128)S(1)} custom-call(f32[2,128,128]{2,1,0:T(8,128)S(1)} %get-tuple-element.10), custom_call_target="InvertDiagBlocksLowerTriangular" | custom-call | tf_op jit(solution)/shard_map/triangular_solve | solution.py:22
  334.3 0.7 fusion
  335.1 1.2 convolution_subtract_fusion
  336.3 0.7 fusion.3
  337.0 20.3 %fusion.9 = f32[2048,256]{1,0:T(8,128)} fusion(f32[1280,2048]{1,0:T(8,128)} %multiply_add_fusion, f32[1280,128]{0,1:T(8,128)S(1)} %fusion.3, f32[1280,128]{0,1:T(8,128)S(1)} %fusion), kind=kOutput, calls=%fused_computation.36 | convolution fusion | flops 8053391360 | bytes 13893632 | tf_op jit(solution)/shard_map/dot_general | solution.py:15
  357.3 0.0 reduce-scatter.2.cloned.1.call-update
  357.4 0.0 all-reduce.6.cloned.1.call-start
  357.4 31.3 %reduce-scatter.2.cloned.1.call-done = f32[512,256]{1,0:T(8,128)} async-done(((f32[2048,256]{1,0:T(8,128)}), f32[512,256]{1,0:T(8,128)}) %reduce-scatter.2.cloned.1.call-update) | async-done | bytes 524304 | tf_op jit(solution)/shard_map/reduce_scatter | solution.py:45
  388.7 0.0 all-gather.10.cloned.1.call-start
  388.8 75.9 %all-reduce.6.cloned.1.call-done = f32[512,256]{1,0:T(8,128)} async-done(((f32[512,256]{1,0:T(8,128)}), f32[512,256]{1,0:T(8,128)}) %all-reduce.6.cloned.1.call-update) | async-done | bytes 524304 | tf_op jit(solution)/shard_map/psum | solution.py:48
  464.7 1.1 multiply_reduce_fusion
  465.8 5.9 %psum.23 = f32[1,256]{1,0:T(1,128)S(1)} all-reduce(f32[1,256]{1,0:T(1,128)S(1)} %bitcast.41), channel_id=1, replica_groups=mesh['dp'=8,'tensor'=4] {'tensor'}, use_global_device_ids=true, to_apply=%region_9.10 | all-reduce | flops 256 | bytes 2048 | tf_op jit(solution)/shard_map/psum | solution.py:49
  471.7 2.0 broadcast_multiply_fusion.1
  473.7 0.1 pad_maximum_fusion
  473.8 1.5 copy.9
  475.3 14.7 %all-gather.10.cloned.1.call-done = bf16[2048,256]{1,0:T(8,128)(2,1)} async-done(((bf16[512,256]{1,0:T(8,128)(2,1)}), bf16[2048,256]{1,0:T(8,128)(2,1)}) %all-gather.10.cloned.1.call-update) | async-done | bytes 1048592 | tf_op jit(solution)/shard_map/all_gather | solution.py:54
  490.0 17.1 %multiply_subtract_fusion = f32[1280,2048]{1,0:T(8,128)} fusion(f32[1280,2048]{1,0:T(8,128)} %multiply_add_fusion, bf16[2048,256]{1,0:T(8,128)(2,1)} %all-gather.10.cloned.1.call-done, f32[1280,128]{0,1:T(8,128)} %copy-done.2, f32[1280,128]{0,1:T(8,128)S(1)} %fusion), kind=kOutput, calls=%fused_computation.2 | convolution fusion | flops 8058634240 | bytes 23330816 | tf_op jit(solution)/shard_map/dot_general | solution.py:52
  (19 shorter events, 0.2 us)
Async XLA Ops:
  7.2 39.6 %copy-start = (bf16[1024,1280]{1,0:T(8,128)(2,1)S(1)}, bf16[1024,1280]{1,0:T(8,128)(2,1)}, u32[]{:S(2)}) copy-start(bf16[1024,1280]{1,0:T(8,128)(2,1)} %param.4) | copy-start | bytes 7864324
  7.2 39.6 %all-gather.6.cloned.1.call-start = ((), (), s32[]{:S(2)}) async-start(), calls=%async_computation.1 | async-start | bytes 5242880 | tf_op jit(solution)/shard_map/all_gather | solution.py:29
  7.9 63.0 %all-gather.8.cloned.1.call-start = ((), (), s32[]{:S(2)}) async-start(), calls=%async_computation.2 | async-start | bytes 2621440 | tf_op jit(solution)/shard_map/all_gather | solution.py:37
  8.7 225.4 %all-gather.12.cloned.1.call-start = ((), (), s32[]{:S(2)}) async-start(), calls=%async_computation.7 | async-start | bytes 11796480 | tf_op jit(solution)/shard_map/all_gather | solution.py:10
  83.4 189.1 %all-reduce.4.cloned.1.call-start = ((), (), s32[]{:S(2)}) async-start(), calls=%async_computation.3 | async-start | bytes 524288 | tf_op jit(solution)/shard_map/psum | solution.py:42
  241.9 146.8 %reduce-scatter.2.cloned.1.call-start = ((), (), s32[]{:S(2)}) async-start(), calls=%async_computation.4 | async-start | bytes 2621440 | tf_op jit(solution)/shard_map/reduce_scatter | solution.py:45
  337.0 136.7 %copy-start.2 = (f32[1280,128]{0,1:T(8,128)}, f32[1280,128]{0,1:T(8,128)S(1)}, u32[]{:S(2)}) copy-start(f32[1280,128]{0,1:T(8,128)S(1)} %fusion.3) | copy-start | bytes 1966084
  357.4 107.3 %all-reduce.6.cloned.1.call-start = ((), (), s32[]{:S(2)}) async-start(), calls=%async_computation.5 | async-start | bytes 1048576 | tf_op jit(solution)/shard_map/psum | solution.py:48
  388.7 101.3 %all-gather.10.cloned.1.call-start = ((), (), s32[]{:S(2)}) async-start(), calls=%async_computation.6 | async-start | bytes 1310720 | tf_op jit(solution)/shard_map/all_gather | solution.py:54
  490.0 17.1 %copy-start.1 = (bf16[1024,1280]{1,0:T(8,128)(2,1)S(1)}, bf16[1024,1280]{1,0:T(8,128)(2,1)}, u32[]{:S(2)}) copy-start(bf16[1024,1280]{1,0:T(8,128)(2,1)} %param.4) | copy-start | bytes 7864324
Sparse Core Ops, SparseCore 0:
  9.5 37.1 all-gather.5
  48.3 22.5 all-gather.7
  83.5 150.5 all-gather.11
  242.0 30.4 all-reduce.3
  357.5 31.1 reduce-scatter.1
  392.0 72.6 all-reduce.5
  473.8 16.1 all-gather.9
